TPU v7x, 32 devices: a whole 2x2x4 slice. The times are simulated.
32 devices in a mesh: seq: 4 (over z), wt: 8 (over y, x, core).
Axes of the slice: x: 2, y: 2, z: 4, core: 2. Of those that a mesh axis runs over, the one named last changes fastest.
Arguments:
- tokens: bfloat16 [8, 512, 2048], P('wt', 'seq'), may hold values from -6 to 6
- cotangent: bfloat16 [8, 512, 2048], P('wt', 'seq'), may hold values from -6 to 6
- segment_ids: int32 [8, 512], P('wt'), may hold values from 0 to 1, never falling along the last dimension, each value on 1 to 320 neighbouring positions
- expert_routes: int32 [8, 512, 8], P('wt', 'seq'), may hold values from 0 to 15, all different within a row; in each aligned block of 128 rows (0 to 127, 128 to 255, ..., all dimensions but the last counted through in order) at most 128 rows name the same one
- w_qkv: bfloat16 [2048, 6144], P('wt'), may hold values from -0.125 to 0.125
- w_out: bfloat16 [2048, 2048], P('wt'), may hold values from -2 to 2
- w_router: bfloat16 [2048, 16], P('wt'), may hold values from -0.0625 to 0.0625
- w_gate_up: bfloat16 [16, 2048, 2048], P('seq', 'wt'), may hold values from -0.125 to 0.125
- w_down: bfloat16 [16, 1024, 2048], P('seq', 'wt'), may hold values from -0.75 to 0.75
- attn_gain: bfloat16 [2048], P('wt'), may hold values from 0.5 to 1.5
- ffn_gain: bfloat16 [2048], P('wt'), may hold values from 0.5 to 1.5
- q_gain: bfloat16 [128], P('wt'), may hold values from 0.5 to 1.5
- k_gain: bfloat16 [128], P('wt'), may hold values from 0.5 to 1.5
Outputs:
- output: bfloat16 [8, 512, 2048], P('wt', 'seq')
- tokens_grad: float32 [8, 512, 2048], P('wt', 'seq')
- w_qkv_grad: float32 [2048, 6144], P('wt')
- w_out_grad: float32 [2048, 2048], P('wt')
- w_router_grad: float32 [2048, 16], P('wt')
- w_gate_up_grad: float32 [16, 2048, 2048], P('seq', 'wt')
- w_down_grad: float32 [16, 1024, 2048], P('seq', 'wt')
- attn_gain_grad: float32 [2048], P('wt')
- ffn_gain_grad: float32 [2048], P('wt')
- q_gain_grad: float32 [128], P('wt')
- k_gain_grad: float32 [128], P('wt')
Inputs may be any that keep to these rules, and one draw needn't show every extreme that they name: `segment_ids`: along a sequence the segment numbers never fall; each of the 2 documents spans 1 to 320 positions. `expert_routes`: A token names 8 different experts; among the 128 tokens of one device no expert is named more than 128 times, a bound that some block reaches.
All inputs are finite; a program needn't handle non-finite values.
Results may differ from a plain program's by a relative error of at most 0.028.
Values may be sent and summed in bfloat16 or wider, within the bound.
A program may use at most 512 MiB of HBM per device.

v0:
```python
import jax
import jax.numpy as jnp
import numpy as np
from jax import lax
from jax.sharding import PartitionSpec as P

H = 16
HD = 128
FF = 1024
EPS = 1e-06
THETA = 50000.0
NEG = -1e30
LANES = 128
BF = jnp.bfloat16
F32 = jnp.float32


def normalize(values):
    factor = lax.rsqrt(jnp.mean(values * values, axis=-1, keepdims=True) + EPS)
    return (values * factor, factor)


def norm_back(grad_normed, normed_values, factor):
    return factor * (
        grad_normed - normed_values * jnp.mean(grad_normed * normed_values, axis=-1, keepdims=True)
    )


def rope_tables(length):
    half = HD // 2
    freq = THETA ** (-jnp.arange(half, dtype=F32) * 2.0 / HD)
    angle = jnp.arange(length, dtype=F32)[:, None] * freq[None, :]
    return (jnp.cos(angle)[:, None, :], jnp.sin(angle)[:, None, :])


def rotate(values, cosine, sine):
    half = values.shape[-1] // 2
    first = values[..., :half]
    second = values[..., half:]
    return jnp.concatenate(
        [first * cosine - second * sine, second * cosine + first * sine], axis=-1
    )


def dot(left, right, dims):
    return lax.dot_general(left, right, (dims, ((), ())), preferred_element_type=F32)


def nn(left, right):
    return dot(left, right, ((1,), (0,)))


def nt(left, right):
    return dot(left, right, ((1,), (1,)))


def tn(left, right):
    return dot(left, right, ((0,), (0,)))


def split_two(values):
    high = values.astype(BF)
    low = (values - high.astype(F32)).astype(BF)
    return (high, low)


def body(
    tokens,
    cotangent,
    segment_ids,
    expert_routes,
    w_qkv,
    w_out,
    w_router,
    w_gate_up,
    w_down,
    attn_gain,
    ffn_gain,
    q_gain,
    k_gain,
):
    seq_total = lax.axis_size("seq")
    wt_total = lax.axis_size("wt")
    seq_me = lax.axis_index("seq")
    rows = tokens.shape[1]
    model = tokens.shape[2]
    length = rows * seq_total
    shard = w_qkv.shape[0]
    local_experts = w_gate_up.shape[0]
    experts = w_router.shape[1]
    heads = H // seq_total
    cols = 3 * heads * HD
    gain_part = q_gain.shape[0]
    tokens_all = lax.all_gather(tokens[0], "seq", axis=0, tiled=True)
    routes_all = lax.all_gather(expert_routes[0], "seq", axis=0, tiled=True)
    w_here = lax.dynamic_slice_in_dim(
        w_qkv.reshape(shard, 3, seq_total, heads * HD), seq_me, 1, axis=2
    ).reshape(shard, cols)
    small = jnp.concatenate(
        [
            w_router,
            attn_gain[:, None],
            ffn_gain[:, None],
            jnp.pad(q_gain, (0, shard - gain_part))[:, None],
            jnp.pad(k_gain, (0, shard - gain_part))[:, None],
        ],
        axis=1,
    )
    small = jnp.pad(small, ((0, 0), (0, LANES - small.shape[1])))
    qkv_full = lax.all_gather(jnp.concatenate([w_here, small], axis=1), "wt", axis=0, tiled=True)
    out_full = lax.all_gather(w_out, "wt", axis=0, tiled=True)
    grad_all = lax.all_gather(cotangent[0], "seq", axis=0, tiled=True)
    expert_full = [
        lax.all_gather(jnp.concatenate([w_gate_up[e], w_down[e]], axis=0), "wt", axis=0)
        for e in range(local_experts)
    ]
    small_full = qkv_full[:, cols:]
    router_full = small_full[:, :experts]
    picker = np.zeros((8, LANES), np.float32)
    for row in range(4):
        picker[row, experts + row] = 1.0
    gain_rows = nt(jnp.asarray(picker, BF), small_full)
    gain_attn = gain_rows[0]
    gain_ffn = gain_rows[1]
    gain_query = gain_rows[2].reshape(wt_total, shard)[:, :gain_part].reshape(HD)
    gain_key = gain_rows[3].reshape(wt_total, shard)[:, :gain_part].reshape(HD)
    segments = segment_ids[0]
    same = segments[:, None] == segments[None, :]
    cosine, sine = rope_tables(length)
    normed_all, _ = normalize(tokens_all.astype(F32))
    hidden = (normed_all * gain_attn).astype(BF)
    projected = nn(hidden, qkv_full)[:, :cols].reshape(length, 3, heads, HD)
    normed_q, factor_q = normalize(projected[:, 0])
    normed_k, factor_k = normalize(projected[:, 1])
    queries = jnp.swapaxes(rotate(normed_q * gain_query, cosine, sine).astype(BF), 0, 1)
    keys = jnp.swapaxes(rotate(normed_k * gain_key, cosine, sine).astype(BF), 0, 1)
    values = jnp.swapaxes(projected[:, 2].astype(BF), 0, 1)
    scale = HD ** (-0.5)

    def bmm(left, right, dims):
        return lax.dot_general(left, right, (dims, ((0,), (0,))), preferred_element_type=F32)

    logits = jnp.where(same[None], bmm(queries, keys, ((2,), (2,))) * scale, NEG)
    powers = jnp.exp(logits - jnp.max(logits, axis=-1, keepdims=True))
    weights = powers / jnp.sum(powers, axis=-1, keepdims=True)
    weights_low = weights.astype(BF)
    attended = bmm(weights_low, values, ((2,), (1,))).astype(BF)
    merged = lax.all_to_all(
        jnp.swapaxes(attended, 0, 1), "seq", split_axis=0, concat_axis=1, tiled=True
    ).reshape(rows, H * HD)
    inputs = tokens[0].astype(F32)
    residual = inputs + nn(merged, out_full)
    normed_f, factor_f = normalize(residual)
    hidden_own = (normed_f * gain_ffn).astype(BF)
    hidden_ffn = lax.all_gather(hidden_own, "seq", axis=0, tiled=True)
    chances = jax.nn.softmax(nn(hidden_ffn, router_full), axis=-1)
    expert_ids = jnp.arange(experts, dtype=jnp.int32)
    routed = jnp.any(routes_all[:, :, None] == expert_ids[None, None, :], axis=1)
    picked = jnp.where(routed, chances, 0.0)
    picked_total = jnp.sum(picked, axis=1, keepdims=True)
    gates = picked / picked_total
    gates_here = lax.dynamic_slice_in_dim(gates, seq_me * local_experts, local_experts, axis=1)
    out_part = jnp.zeros((length, model), F32)
    grad_hidden_part = jnp.zeros((length, model), F32)
    gate_grads = []
    expert_grads = []
    for e in range(local_experts):
        gate = gates_here[:, e : e + 1]
        gate_up = expert_full[e][:, : model // wt_total].reshape(model, 2 * FF)
        down = expert_full[e][:, model // wt_total :].reshape(FF, model)
        before = nn(hidden_ffn, gate_up)
        gate_part = before[:, :FF]
        up_part = before[:, FF:]
        sigmoid_gate = jax.nn.sigmoid(gate_part)
        silu_gate = gate_part * sigmoid_gate
        activated = silu_gate * up_part
        scaled = (gate * activated).astype(BF)
        grad_act = nt(grad_all, down)
        gate_grads.append(jnp.sum(grad_act * activated, axis=1, keepdims=True))
        grad_act = grad_act * gate
        grad_gate = grad_act * up_part * sigmoid_gate * (1.0 + gate_part * (1.0 - sigmoid_gate))
        grad_up = grad_act * silu_gate
        grad_before = jnp.concatenate([grad_gate, grad_up], axis=-1).astype(BF)
        out_part = out_part + nn(scaled, down)
        grad_hidden_part = grad_hidden_part + nt(grad_before, gate_up)
        gate_up_grad = tn(hidden_ffn, grad_before).astype(BF)
        down_grad = tn(scaled, grad_all).astype(BF)
        joined = jnp.concatenate(
            [
                gate_up_grad.reshape(wt_total, model // wt_total, 2 * FF),
                down_grad.reshape(wt_total, FF // wt_total, model),
            ],
            axis=1,
        )
        expert_grads.append(
            lax.psum_scatter(joined, "wt", scatter_dimension=0, tiled=False).astype(F32)
        )
    gate_up_out = jnp.stack([g[: model // wt_total] for g in expert_grads])
    down_out = jnp.stack([g[model // wt_total :] for g in expert_grads])
    gate_grad_part = jnp.concatenate(gate_grads, axis=1)
    gate_high, gate_low = split_two(gate_grad_part)

    def spread(part):
        wide = jnp.zeros((length, experts), BF)
        return lax.dynamic_update_slice(wide, part, (0, seq_me * local_experts))

    returned = lax.psum_scatter(
        jnp.concatenate([grad_hidden_part.astype(BF), spread(gate_high), spread(gate_low)], axis=1),
        "seq",
        scatter_dimension=0,
        tiled=True,
    ).astype(F32)
    grad_hidden = returned[:, :model]
    gate_grad = returned[:, model : model + experts] + returned[:, model + experts :]
    moe_out = lax.psum_scatter(out_part.astype(BF), "seq", scatter_dimension=0, tiled=True).astype(
        F32
    )
    output = (residual + moe_out).astype(BF)

    def own(full):
        return lax.dynamic_slice_in_dim(full, seq_me * rows, rows, axis=0)

    chances_own = own(chances)
    routed_own = own(routed)
    gates_own = own(gates)
    inner_gate = jnp.sum(gate_grad * gates_own, axis=1, keepdims=True)
    grad_chances = jnp.where(routed_own, (gate_grad - inner_gate) / own(picked_total), 0.0)
    grad_logits = (
        chances_own * (grad_chances - jnp.sum(grad_chances * chances_own, axis=1, keepdims=True))
    ).astype(BF)
    grad_hidden = grad_hidden + nt(grad_logits, router_full)
    router_grad = tn(hidden_own, grad_logits)
    ffn_gain_grad = jnp.sum(grad_hidden * normed_f, axis=0)
    grad_residual = cotangent[0].astype(F32) + norm_back(grad_hidden * gain_ffn, normed_f, factor_f)
    grad_branch = grad_residual.astype(BF)
    grad_merged = nt(grad_branch, out_full).astype(BF).reshape(rows, H, HD)
    grad_heads = jnp.swapaxes(
        lax.all_to_all(grad_merged, "seq", split_axis=1, concat_axis=0, tiled=True), 0, 1
    )
    out_grad = lax.psum_scatter(
        tn(merged, grad_branch).astype(BF), "wt", scatter_dimension=0, tiled=True
    )
    out_grad = lax.psum(out_grad, "seq").astype(F32)
    grad_weights = bmm(grad_heads, values, ((2,), (2,)))
    inner = jnp.sum(weights * grad_weights, axis=-1, keepdims=True)
    grad_scores = (weights * (grad_weights - inner)).astype(BF)
    grad_q = jnp.swapaxes(bmm(grad_scores, keys, ((2,), (1,))), 0, 1) * scale
    grad_k = jnp.swapaxes(bmm(grad_scores, queries, ((1,), (1,))), 0, 1) * scale
    grad_v = jnp.swapaxes(bmm(weights_low, grad_heads, ((1,), (1,))), 0, 1)
    grad_q_normed = rotate(grad_q, cosine, -sine)
    grad_k_normed = rotate(grad_k, cosine, -sine)
    q_gain_grad = jnp.sum(grad_q_normed * normed_q, axis=(0, 1))
    k_gain_grad = jnp.sum(grad_k_normed * normed_k, axis=(0, 1))
    grad_q_raw = norm_back(grad_q_normed * gain_query, normed_q, factor_q)
    grad_k_raw = norm_back(grad_k_normed * gain_key, normed_k, factor_k)
    grad_projected = (
        jnp.stack([grad_q_raw, grad_k_raw, grad_v], axis=1).reshape(length, cols).astype(BF)
    )
    qkv_grad = tn(hidden, grad_projected)
    grad_normed_part = nt(jnp.pad(grad_projected, ((0, 0), (0, LANES))), qkv_full)
    attn_gain_grad = jnp.sum(grad_normed_part * normed_all, axis=0)
    grad_normed_own = lax.psum_scatter(
        grad_normed_part.astype(BF), "seq", scatter_dimension=0, tiled=True
    ).astype(F32)
    normed_a, factor_a = normalize(inputs)
    tokens_grad = grad_residual + norm_back(grad_normed_own * gain_attn, normed_a, factor_a)

    def gain_column(vector):
        return jnp.pad(
            vector.reshape(wt_total, gain_part), ((0, 0), (0, shard - gain_part))
        ).reshape(model, 1)

    small_grad = jnp.concatenate(
        [
            router_grad,
            attn_gain_grad[:, None],
            ffn_gain_grad[:, None],
            gain_column(q_gain_grad),
            gain_column(k_gain_grad),
        ],
        axis=1,
    )
    small_grad = jnp.pad(small_grad, ((0, 0), (0, LANES - small_grad.shape[1])))
    scattered = lax.psum_scatter(
        jnp.concatenate([qkv_grad, small_grad], axis=1).astype(BF),
        "wt",
        scatter_dimension=0,
        tiled=True,
    )
    collected = lax.all_gather(scattered, "seq", axis=0).astype(F32)
    qkv_out = (
        collected[:, :, :cols]
        .reshape(seq_total, shard, 3, heads * HD)
        .transpose(1, 2, 0, 3)
        .reshape(shard, 3 * H * HD)
    )
    small_out = jnp.sum(collected[:, :, cols:], axis=0)
    return (
        output[None],
        tokens_grad[None],
        qkv_out,
        out_grad,
        small_out[:, :experts],
        gate_up_out,
        down_out,
        small_out[:, experts],
        small_out[:, experts + 1],
        small_out[:gain_part, experts + 2],
        small_out[:gain_part, experts + 3],
    )


def solution(mesh):
    in_specs = (
        P("wt", "seq", None),
        P("wt", "seq", None),
        P("wt", None),
        P("wt", "seq", None),
        P("wt", None),
        P("wt", None),
        P("wt", None),
        P("seq", "wt", None),
        P("seq", "wt", None),
        P("wt"),
        P("wt"),
        P("wt"),
        P("wt"),
    )
    out_specs = (
        P("wt", "seq", None),
        P("wt", "seq", None),
        P("wt", None),
        P("wt", None),
        P("wt", None),
        P("seq", "wt", None),
        P("seq", "wt", None),
        P("wt"),
        P("wt"),
        P("wt"),
        P("wt"),
    )
    return jax.shard_map(body, mesh=mesh, in_specs=in_specs, out_specs=out_specs, check_vma=False)
```

profile of v0, /device:TPU:0, one launch (start us, length us, event | category | flops | bytes accessed | tf_op | source)
XLA Modules:
  0.0 1457.3 jit_solution(14407658807051301885)
XLA Ops:
  18.4 39.6 %all-gather.25.cloned.1.call-done = bf16[1,512,2048]{2,1,0:T(8,128)(2,1)} async-done(((bf16[1,128,2048]{2,1,0:T(8,128)(2,1)}), bf16[1,512,2048]{2,1,0:T(8,128)(2,1)}) %all-gather.25.cloned.1.call-update) | async-done | bytes 2097168 | tf_op jit(solution)/shard_map/all_gather | solution.py:94
  60.1 48.1 %all-gather.19.cloned.1.call-done = bf16[2048,1664]{0,1:T(8,128)(2,1)} async-done(((bf16[256,1664]{0,1:T(8,128)(2,1)}), bf16[2048,1664]{0,1:T(8,128)(2,1)}) %all-gather.19.cloned.1.call-update) | async-done | bytes 6815760 | tf_op jit(solution)/shard_map/all_gather | solution.py:110
  110.0 8.6 fusion.3
  133.7 19.4 %all_to_all.33 = bf16[512,4,128]{2,1,0:T(4,128)(2,1)S(1)} all-to-all(bf16[512,4,128]{2,1,0:T(4,128)(2,1)S(1)} %copy.163), channel_id=1, replica_groups=mesh['seq'=4,'wt'=8] {'seq'}, dimensions={0} | all-to-all | bytes 1048576 | tf_op jit(solution)/shard_map/all_to_all | solution.py:148
  153.4 10.9 all-gather.21.cloned.1.call-done
  182.9 13.9 all-gather.1
  197.0 20.3 %all-gather.23.cloned.1.call-done = bf16[512,2048]{1,0:T(8,128)(2,1)} async-done(((bf16[128,2048]{1,0:T(8,128)(2,1)}), bf16[512,2048]{1,0:T(8,128)(2,1)}) %all-gather.23.cloned.1.call-update) | async-done | bytes 2097168 | tf_op jit(solution)/shard_map/all_gather | solution.py:155
  222.4 68.0 %all-gather.31.cloned.1.call-done = bf16[3072,2048]{1,0:T(8,128)(2,1)} async-done(((bf16[384,2048]{1,0:T(8,128)(2,1)}), bf16[3072,2048]{1,0:T(8,128)(2,1)}) %all-gather.31.cloned.1.call-update) | async-done | bytes 12582928 | tf_op jit(solution)/shard_map/all_gather | solution.py:114
  304.3 60.5 %all-gather.27.cloned.1.call-done = bf16[3072,2048]{1,0:T(8,128)(2,1)} async-done(((bf16[384,2048]{1,0:T(8,128)(2,1)}), bf16[3072,2048]{1,0:T(8,128)(2,1)}) %all-gather.27.cloned.1.call-update) | async-done | bytes 12582928 | tf_op jit(solution)/shard_map/all_gather | solution.py:114
  378.5 60.2 %all-gather.29.cloned.1.call-done = bf16[3072,2048]{1,0:T(8,128)(2,1)} async-done(((bf16[384,2048]{1,0:T(8,128)(2,1)}), bf16[3072,2048]{1,0:T(8,128)(2,1)}) %all-gather.29.cloned.1.call-update) | async-done | bytes 12582928 | tf_op jit(solution)/shard_map/all_gather | solution.py:114
  452.5 60.1 %all-gather.33.cloned.1.call-done = bf16[3072,2048]{1,0:T(8,128)(2,1)} async-done(((bf16[384,2048]{1,0:T(8,128)(2,1)}), bf16[3072,2048]{1,0:T(8,128)(2,1)}) %all-gather.33.cloned.1.call-update) | async-done | bytes 12582928 | tf_op jit(solution)/shard_map/all_gather | solution.py:114
  526.1 9.6 fusion.110
  559.9 9.1 multiply_convert_fusion.4
  583.8 10.7 fusion.39
  594.5 9.7 fusion.41
  611.5 12.3 add_convert_fusion
  642.1 30.1 %reduce-scatter.12.cloned.1.call-done = bf16[128,2080]{1,0:T(8,128)(2,1)} async-done(((bf16[512,2080]{1,0:T(8,128)(2,1)}), bf16[128,2080]{1,0:T(8,128)(2,1)}) %reduce-scatter.12.cloned.1.call-update) | async-done | bytes 532496 | tf_op jit(solution)/shard_map/reduce_scatter | solution.py:207
  677.6 40.4 %reduce-scatter.10.cloned.1.call-done = bf16[128,2048]{1,0:T(8,128)(2,1)} async-done(((bf16[512,2048]{1,0:T(8,128)(2,1)}), bf16[128,2048]{1,0:T(8,128)(2,1)}) %reduce-scatter.10.cloned.1.call-update) | async-done | bytes 524304 | tf_op jit(solution)/shard_map/reduce_scatter | solution.py:215
  737.4 14.1 all-to-all-done.1
  768.3 9.8 fusion.8
  806.8 9.1 pad_maximum_fusion.3
  826.3 9.1 pad_maximum_fusion.2
  845.9 9.1 pad_maximum_fusion.1
  865.3 9.0 pad_maximum_fusion
  875.6 35.4 %reduce-scatter.14.cloned.1.call-done = bf16[128,2048]{1,0:T(8,128)(2,1)} async-done(((bf16[512,2048]{1,0:T(8,128)(2,1)}), bf16[128,2048]{1,0:T(8,128)(2,1)}) %reduce-scatter.14.cloned.1.call-update) | async-done | bytes 524304 | tf_op jit(solution)/shard_map/reduce_scatter | solution.py:262
  914.8 49.5 %all-reduce.9.cloned.1.call-done = bf16[256,2048]{1,0:T(8,128)(2,1)} async-done(((bf16[256,2048]{1,0:T(8,128)(2,1)}), bf16[256,2048]{1,0:T(8,128)(2,1)}) %all-reduce.9.cloned.1.call-update) | async-done | bytes 1048592 | tf_op jit(solution)/shard_map/psum | solution.py:243
  967.1 92.2 %reduce-scatter.26.cloned.1.call-done = bf16[1,384,2048]{2,1,0:T(8,128)(2,1)} async-done(((bf16[8,384,2048]{2,1,0:T(8,128)(2,1)}), bf16[1,384,2048]{2,1,0:T(8,128)(2,1)}) %reduce-scatter.26.cloned.1.call-update) | async-done | bytes 1572880 | tf_op jit(solution)/shard_map/reduce_scatter | solution.py:196
  1061.1 93.8 %reduce-scatter.24.cloned.1.call-done = bf16[1,384,2048]{2,1,0:T(8,128)(2,1)} async-done(((bf16[8,384,2048]{2,1,0:T(8,128)(2,1)}), bf16[1,384,2048]{2,1,0:T(8,128)(2,1)}) %reduce-scatter.24.cloned.1.call-update) | async-done | bytes 1572880 | tf_op jit(solution)/shard_map/reduce_scatter | solution.py:196
  1158.9 91.7 %reduce-scatter.22.cloned.1.call-done = bf16[1,384,2048]{2,1,0:T(8,128)(2,1)} async-done(((bf16[8,384,2048]{2,1,0:T(8,128)(2,1)}), bf16[1,384,2048]{2,1,0:T(8,128)(2,1)}) %reduce-scatter.22.cloned.1.call-update) | async-done | bytes 1572880 | tf_op jit(solution)/shard_map/reduce_scatter | solution.py:196
  1254.6 91.8 %reduce-scatter.20.cloned.1.call-done = bf16[1,384,2048]{2,1,0:T(8,128)(2,1)} async-done(((bf16[8,384,2048]{2,1,0:T(8,128)(2,1)}), bf16[1,384,2048]{2,1,0:T(8,128)(2,1)}) %reduce-scatter.20.cloned.1.call-update) | async-done | bytes 1572880 | tf_op jit(solution)/shard_map/reduce_scatter | solution.py:196
  1356.2 59.4 %all-gather.37.cloned.1.call-done = bf16[1024,1664]{0,1:T(8,128)(2,1)} async-done(((bf16[256,1664]{0,1:T(8,128)(2,1)}), bf16[1024,1664]{0,1:T(8,128)(2,1)}) %all-gather.37.cloned.1.call-update) | async-done | bytes 3407888 | tf_op jit(solution)/shard_map/all_gather | solution.py:290
  1433.3 8.7 copy.187
  (411 shorter events, 327.3 us)
Async XLA Ops:
  7.2 50.8 %all-gather.25.cloned.1.call-start = ((), (), s32[]{:S(2)}) async-start(), calls=%async_computation.24 | async-start | bytes 2621440 | tf_op jit(solution)/shard_map/all_gather | solution.py:94
  7.9 100.2 %all-gather.19.cloned.1.call-start = ((), (), s32[]{:S(2)}) async-start(), calls=%async_computation.11 | async-start | bytes 7667712 | tf_op jit(solution)/shard_map/all_gather | solution.py:110
  13.8 94.4 %copy-start.73 = (bf16[8,128]{1,0:T(8,128)(2,1)S(1)}, bf16[8,128]{1,0:T(8,128)(2,1)}, u32[]{:S(2)}) copy-start(bf16[8,128]{1,0:T(8,128)(2,1)} %constant.61.clone) | copy-start | bytes 6148
  14.9 149.4 %all-gather.21.cloned.1.call-start = ((), (), s32[]{:S(2)}) async-start(), calls=%async_computation.12 | async-start | bytes 9437184 | tf_op jit(solution)/shard_map/all_gather | solution.py:111
  15.7 201.6 %all-gather.23.cloned.1.call-start = ((), (), s32[]{:S(2)}) async-start(), calls=%async_computation.13 | async-start | bytes 2621440 | tf_op jit(solution)/shard_map/all_gather | solution.py:155
  18.4 106.9 %copy-start.28 = (f32[512,64]{1,0:T(8,128)}, f32[512,64]{1,0:T(8,128)S(1)}, u32[]{:S(2)}) copy-start(f32[512,64]{1,0:T(8,128)S(1)} %get-tuple-element.77) | copy-start | bytes 393220
  60.1 49.4 %copy-start.74 = (f32[512]{0:T(512)}, f32[512]{0:T(512)S(1)}, u32[]{:S(2)}) copy-start(f32[512]{0:T(512)S(1)} %add_rsqrt_fusion.2) | copy-start | bytes 6148
  109.5 59.8 %copy-start.53 = (f32[1,2048]{1,0:T(1,128)}, f32[1,2048]{1,0:T(1,128)S(1)}, u32[]{:S(2)}) copy-start(f32[1,2048]{1,0:T(1,128)S(1)} %get-tuple-element.73) | copy-start | bytes 24580
  171.2 119.2 %all-gather.31.cloned.1.call-start = ((), (), s32[]{:S(2)}) async-start(), calls=%async_computation.27 | async-start | bytes 14155776 | tf_op jit(solution)/shard_map/all_gather | solution.py:114
  175.8 189.0 %all-gather.27.cloned.1.call-start = ((), (), s32[]{:S(2)}) async-start(), calls=%async_computation.25 | async-start | bytes 14155776 | tf_op jit(solution)/shard_map/all_gather | solution.py:114
  178.2 260.5 %all-gather.29.cloned.1.call-start = ((), (), s32[]{:S(2)}) async-start(), calls=%async_computation.26 | async-start | bytes 14155776 | tf_op jit(solution)/shard_map/all_gather | solution.py:114
  180.8 331.8 %all-gather.33.cloned.1.call-start = ((), (), s32[]{:S(2)}) async-start(), calls=%async_computation.28 | async-start | bytes 14155776 | tf_op jit(solution)/shard_map/all_gather | solution.py:114
  182.1 377.8 %all-gather.35.cloned.1.call-start = ((), (), s32[]{:S(2)}) async-start(), calls=%async_computation.29 | async-start | bytes 2621440 | tf_op jit(solution)/shard_map/all_gather | solution.py:112
  182.8 489.3 %reduce-scatter.12.cloned.1.call-start = ((), (), s32[]{:S(2)}) async-start(), calls=%async_computation.15 | async-start | bytes 2785280 | tf_op jit(solution)/shard_map/reduce_scatter | solution.py:207
  197.0 101.9 %copy-start.49 = (pred[512,16]{1,0:T(8,128)(4,1)}, pred[512,16]{1,0:T(8,128)(4,1)S(1)}, u32[]{:S(2)}) copy-start(pred[512,16]{1,0:T(8,128)(4,1)S(1)} %copy.167) | copy-start | bytes 24580
  220.2 78.6 %copy-start.64 = (f32[512]{0:T(512)}, f32[512]{0:T(512)S(1)}, u32[]{:S(2)}) copy-start(f32[512]{0:T(512)S(1)} %get-tuple-element.25) | copy-start | bytes 6148
  583.2 53.8 %copy-start.78 = (bf16[512,1024]{1,0:T(8,128)(2,1)}, bf16[512,1024]{1,0:T(8,128)(2,1)S(1)}, u32[]{:S(2)}) copy-start(bf16[512,1024]{1,0:T(8,128)(2,1)S(1)} %get-tuple-element.39) | copy-start | bytes 3145732
  626.7 91.3 %reduce-scatter.10.cloned.1.call-start = ((), (), s32[]{:S(2)}) async-start(), calls=%async_computation.14 | async-start | bytes 2621440 | tf_op jit(solution)/shard_map/reduce_scatter | solution.py:215
  637.0 37.4 %copy-start.46 = (f32[512,16]{1,0:T(8,128)S(1)}, f32[512,16]{1,0:T(8,128)}, u32[]{:S(2)}) copy-start(f32[512,16]{1,0:T(8,128)} %copy-done.45) | copy-start | bytes 98308
  640.8 34.6 %copy-start.71 = (f32[128]{0:T(128)S(1)}, f32[128]{0:T(128)}, u32[]{:S(2)}) copy-start(f32[128]{0:T(128)} %copy-done.70) | copy-start | bytes 1540
  640.8 77.2 %copy-start.35 = (bf16[1,128,2048]{2,1,0:T(8,128)(2,1)S(1)}, bf16[1,128,2048]{2,1,0:T(8,128)(2,1)}, u32[]{:S(2)}) copy-start(bf16[1,128,2048]{2,1,0:T(8,128)(2,1)} %param.15) | copy-start | bytes 1572868
  640.9 156.3 %reduce-scatter.18.cloned.1.call-start = ((), (), s32[]{:S(2)}) async-start(), calls=%async_computation.18 | async-start | bytes 9437184 | tf_op jit(solution)/shard_map/reduce_scatter | solution.py:240
  674.3 46.2 %copy-start.9 = (bf16[128,4,4,128]{0,3,2,1:T(8,128)(2,1)S(1)}, bf16[128,4,4,128]{0,3,2,1:T(8,128)(2,1)}, u32[]{:S(2)}) copy-start(bf16[128,4,4,128]{0,3,2,1:T(8,128)(2,1)} %copy-done.8) | copy-start | bytes 1572868
  733.6 17.9 %all-to-all-start.1 = ((bf16[128,16,128]{2,0,1:T(8,128)(2,1)}), bf16[128,16,128]{2,0,1:T(8,128)(2,1)S(1)}, u32[]{:S(2)}, u32[]{:S(2)}) async-start(bf16[128,16,128]{2,0,1:T(8,128)(2,1)} %bitcast.275), calls=%async_computation.3 | async-start | bytes 1048576 | tf_op jit(solution)/shard_map/all_to_all | solution.py:238
  737.1 137.4 %reduce-scatter.16.cloned.1.call-start = ((), (), s32[]{:S(2)}) async-start(), calls=%async_computation.17 | async-start | bytes 7667712 | tf_op jit(solution)/shard_map/reduce_scatter | solution.py:284
  791.9 119.1 %reduce-scatter.14.cloned.1.call-start = ((), (), s32[]{:S(2)}) async-start(), calls=%async_computation.16 | async-start | bytes 2621440 | tf_op jit(solution)/shard_map/reduce_scatter | solution.py:262
  792.5 171.9 %all-reduce.9.cloned.1.call-start = ((), (), s32[]{:S(2)}) async-start(), calls=%async_computation.19 | async-start | bytes 2097152 | tf_op jit(solution)/shard_map/psum | solution.py:243
  797.2 262.1 %reduce-scatter.26.cloned.1.call-start = ((), (), s32[]{:S(2)}) async-start(), calls=%async_computation.23 | async-start | bytes 14155776 | tf_op jit(solution)/shard_map/reduce_scatter | solution.py:196
  815.9 339.1 %reduce-scatter.24.cloned.1.call-start = ((), (), s32[]{:S(2)}) async-start(), calls=%async_computation.22 | async-start | bytes 14155776 | tf_op jit(solution)/shard_map/reduce_scatter | solution.py:196
  835.4 415.2 %reduce-scatter.22.cloned.1.call-start = ((), (), s32[]{:S(2)}) async-start(), calls=%async_computation.21 | async-start | bytes 14155776 | tf_op jit(solution)/shard_map/reduce_scatter | solution.py:196
  855.0 491.5 %reduce-scatter.20.cloned.1.call-start = ((), (), s32[]{:S(2)}) async-start(), calls=%async_computation.20 | async-start | bytes 14155776 | tf_op jit(solution)/shard_map/reduce_scatter | solution.py:196
  874.4 541.2 %all-gather.37.cloned.1.call-start = ((), (), s32[]{:S(2)}) async-start(), calls=%async_computation.30 | async-start | bytes 4259840 | tf_op jit(solution)/shard_map/all_gather | solution.py:290
  (95 other events, 575.3 us)
Sparse Core Ops, SparseCore 0:
  9.6 48.3 all-gather.24
  60.4 47.6 all-gather.18
  110.1 54.2 all-gather.20
  171.3 45.9 all-gather.22
  219.6 70.7 all-gather.30
  292.7 71.9 all-gather.26
  366.7 71.9 all-gather.28
  440.6 71.9 all-gather.32
  514.2 45.6 all-gather.34
  626.8 45.2 reduce-scatter.11
  675.0 42.9 reduce-scatter.9
  726.4 70.6 reduce-scatter.17
  800.6 64.0 reduce-scatter.15
  867.4 43.6 reduce-scatter.13
  913.2 51.0 all-reduce.8
  967.7 91.5 reduce-scatter.25
  1062.6 92.2 reduce-scatter.23
  1158.3 92.2 reduce-scatter.21
  1254.1 92.2 reduce-scatter.19
  1347.9 67.6 all-gather.36
where the time goes:
time: 1470 us; the launch traced here: 1460 us
  waiting for transfers between devices  979 us (67%)
  matrix products  200 us (14%)
  local copies, waits for them, and re-layouts  134 us (9%)
  other arithmetic  88.7 us (6%)
  blocking collectives  33.2 us (2%)
  between operations  16 us (1%)
    reduce_scatter x4, waiting for transfers between devices, body(): lax.psum_scatter(joined, 'wt', scatter_dimension=0, tiled=False).astype(F32)  369 us
    all_gather x4, waiting for transfers between devices, body(): lax.all_gather(jnp.concatenate([w_gate_up[e], w_down[e]], axis=0), 'wt',...  249 us
    dot_general x34, matrix products, dot(): lax.dot_general(left, right, (dims, ((), ())), preferred_element_type=F32)  188 us
    all_gather x1, waiting for transfers between devices, body(): collected = lax.all_gather(scattered, 'seq', axis=0).astype(F32)  59.4 us
    psum x1, waiting for transfers between devices, body(): out_grad = lax.psum(out_grad, 'seq').astype(F32)  49.5 us
    all_gather x1, waiting for transfers between devices, body(): lax.all_gather(jnp.concatenate([w_here, small], axis=1), 'wt', axis=0, ti...  48.1 us
    reduce_scatter x1, waiting for transfers between devices, body(): lax.psum_scatter(out_part.astype(BF), 'seq', scatter_dimension=0, tiled=T...  40.4 us
    all_gather x1, waiting for transfers between devices, body(): tokens_all = lax.all_gather(tokens[0], 'seq', axis=0, tiled=True)  39.6 us
  transfers between devices with their start and end apart: 21, of which 20 were waited for; matrix products, arithmetic and copies ran while one was open for 20% of the time, Pallas kernels for 0%

commit v1 on v0

--- a/solution.py
+++ b/solution.py
@@ -145,9 +145,17 @@
     weights = powers / jnp.sum(powers, axis=-1, keepdims=True)
     weights_low = weights.astype(BF)
     attended = bmm(weights_low, values, ((2,), (1,))).astype(BF)
-    merged = lax.all_to_all(
-        jnp.swapaxes(attended, 0, 1), "seq", split_axis=0, concat_axis=1, tiled=True
-    ).reshape(rows, H * HD)
+
+    def measure_group(sample, chip_axis):
+        local_out = jnp.concatenate(
+            lax.all_to_all(
+                jnp.stack(jnp.split(sample, lax.axis_size(chip_axis), 0), 0), chip_axis, 0, 0
+            ),
+            1,
+        )
+        return local_out
+
+    merged = measure_group(jnp.swapaxes(attended, 0, 1), "seq").reshape(rows, H * HD)
     inputs = tokens[0].astype(F32)
     residual = inputs + nn(merged, out_full)
     normed_f, factor_f = normalize(residual)

time: 1470 us -> 1470 us (level)
  no operation moved by 1% of the time
where the time goes in v1:
time: 1470 us; the launch traced here: 1460 us
  waiting for transfers between devices  979 us (67%)
  matrix products  201 us (14%)
  local copies, waits for them, and re-layouts  134 us (9%)
  other arithmetic  88.9 us (6%)
  blocking collectives  33.3 us (2%)
  between operations  16 us (1%)
    reduce_scatter x4, waiting for transfers between devices, body(): lax.psum_scatter(joined, 'wt', scatter_dimension=0, tiled=False).astype(F32)  369 us
    all_gather x4, waiting for transfers between devices, body(): lax.all_gather(jnp.concatenate([w_gate_up[e], w_down[e]], axis=0), 'wt',...  249 us
    dot_general x34, matrix products, dot(): lax.dot_general(left, right, (dims, ((), ())), preferred_element_type=F32)  188 us
    all_gather x1, waiting for transfers between devices, body(): collected = lax.all_gather(scattered, 'seq', axis=0).astype(F32)  59.4 us
    psum x1, waiting for transfers between devices, body(): out_grad = lax.psum(out_grad, 'seq').astype(F32)  49.5 us
    all_gather x1, waiting for transfers between devices, body(): lax.all_gather(jnp.concatenate([w_here, small], axis=1), 'wt', axis=0, ti...  48.1 us
    reduce_scatter x1, waiting for transfers between devices, body(): lax.psum_scatter(out_part.astype(BF), 'seq', scatter_dimension=0, tiled=T...  40.3 us
    all_gather x1, waiting for transfers between devices, body(): tokens_all = lax.all_gather(tokens[0], 'seq', axis=0, tiled=True)  39.6 us
  transfers between devices with their start and end apart: 21, of which 20 were waited for; matrix products, arithmetic and copies ran while one was open for 20% of the time, Pallas kernels for 0%

profile of v1, /device:TPU:0, one launch (start us, length us, event | category | flops | bytes accessed | tf_op | source)
XLA Modules:
  0.0 1457.5 jit_solution(7589946342975081403)
XLA Ops:
  18.4 39.6 %all-gather.25.cloned.1.call-done = bf16[1,512,2048]{2,1,0:T(8,128)(2,1)} async-done(((bf16[1,128,2048]{2,1,0:T(8,128)(2,1)}), bf16[1,512,2048]{2,1,0:T(8,128)(2,1)}) %all-gather.25.cloned.1.call-update) | async-done | bytes 2097168 | tf_op jit(solution)/shard_map/all_gather | solution.py:94
  60.1 48.1 %all-gather.19.cloned.1.call-done = bf16[2048,1664]{0,1:T(8,128)(2,1)} async-done(((bf16[256,1664]{0,1:T(8,128)(2,1)}), bf16[2048,1664]{0,1:T(8,128)(2,1)}) %all-gather.19.cloned.1.call-update) | async-done | bytes 6815760 | tf_op jit(solution)/shard_map/all_gather | solution.py:110
  110.0 8.6 fusion.3
  133.4 19.5 %all_to_all.23 = bf16[4,128,4,128]{3,1,2,0:T(8,128)(2,1)S(1)} all-to-all(bf16[4,128,4,128]{3,1,2,0:T(8,128)(2,1)S(1)} %pad_maximum_fusion.25), channel_id=1, replica_groups=mesh['seq'=4,'wt'=8] {'seq'}, dimensions={0} | all-to-all | bytes 1048576 | tf_op jit(solution)/shard_map/all_to_all | solution.py:151
  153.2 11.2 all-gather.21.cloned.1.call-done
  182.9 13.8 all-gather.1
  196.9 20.4 %all-gather.23.cloned.1.call-done = bf16[512,2048]{1,0:T(8,128)(2,1)} async-done(((bf16[128,2048]{1,0:T(8,128)(2,1)}), bf16[512,2048]{1,0:T(8,128)(2,1)}) %all-gather.23.cloned.1.call-update) | async-done | bytes 2097168 | tf_op jit(solution)/shard_map/all_gather | solution.py:163
  222.5 68.0 %all-gather.31.cloned.1.call-done = bf16[3072,2048]{1,0:T(8,128)(2,1)} async-done(((bf16[384,2048]{1,0:T(8,128)(2,1)}), bf16[3072,2048]{1,0:T(8,128)(2,1)}) %all-gather.31.cloned.1.call-update) | async-done | bytes 12582928 | tf_op jit(solution)/shard_map/all_gather | solution.py:114
  304.3 60.5 %all-gather.27.cloned.1.call-done = bf16[3072,2048]{1,0:T(8,128)(2,1)} async-done(((bf16[384,2048]{1,0:T(8,128)(2,1)}), bf16[3072,2048]{1,0:T(8,128)(2,1)}) %all-gather.27.cloned.1.call-update) | async-done | bytes 12582928 | tf_op jit(solution)/shard_map/all_gather | solution.py:114
  378.5 60.2 %all-gather.29.cloned.1.call-done = bf16[3072,2048]{1,0:T(8,128)(2,1)} async-done(((bf16[384,2048]{1,0:T(8,128)(2,1)}), bf16[3072,2048]{1,0:T(8,128)(2,1)}) %all-gather.29.cloned.1.call-update) | async-done | bytes 12582928 | tf_op jit(solution)/shard_map/all_gather | solution.py:114
  452.5 60.1 %all-gather.33.cloned.1.call-done = bf16[3072,2048]{1,0:T(8,128)(2,1)} async-done(((bf16[384,2048]{1,0:T(8,128)(2,1)}), bf16[3072,2048]{1,0:T(8,128)(2,1)}) %all-gather.33.cloned.1.call-update) | async-done | bytes 12582928 | tf_op jit(solution)/shard_map/all_gather | solution.py:114
  526.1 9.6 fusion.110
  559.9 9.1 multiply_convert_fusion.4
  583.8 10.7 fusion.39
  594.5 9.7 fusion.41
  611.6 12.3 add_convert_fusion
  642.2 30.1 %reduce-scatter.12.cloned.1.call-done = bf16[128,2080]{1,0:T(8,128)(2,1)} async-done(((bf16[512,2080]{1,0:T(8,128)(2,1)}), bf16[128,2080]{1,0:T(8,128)(2,1)}) %reduce-scatter.12.cloned.1.call-update) | async-done | bytes 532496 | tf_op jit(solution)/shard_map/reduce_scatter | solution.py:215
  677.7 40.3 %reduce-scatter.10.cloned.1.call-done = bf16[128,2048]{1,0:T(8,128)(2,1)} async-done(((bf16[512,2048]{1,0:T(8,128)(2,1)}), bf16[128,2048]{1,0:T(8,128)(2,1)}) %reduce-scatter.10.cloned.1.call-update) | async-done | bytes 524304 | tf_op jit(solution)/shard_map/reduce_scatter | solution.py:223
  737.5 14.1 all-to-all-done.1
  768.3 9.8 fusion.8
  806.9 9.1 pad_maximum_fusion.3
  826.5 9.2 pad_maximum_fusion.2
  846.1 9.1 pad_maximum_fusion.1
  865.6 9.0 pad_maximum_fusion
  875.9 35.2 %reduce-scatter.14.cloned.1.call-done = bf16[128,2048]{1,0:T(8,128)(2,1)} async-done(((bf16[512,2048]{1,0:T(8,128)(2,1)}), bf16[128,2048]{1,0:T(8,128)(2,1)}) %reduce-scatter.14.cloned.1.call-update) | async-done | bytes 524304 | tf_op jit(solution)/shard_map/reduce_scatter | solution.py:270
  914.9 49.5 %all-reduce.9.cloned.1.call-done = bf16[256,2048]{1,0:T(8,128)(2,1)} async-done(((bf16[256,2048]{1,0:T(8,128)(2,1)}), bf16[256,2048]{1,0:T(8,128)(2,1)}) %all-reduce.9.cloned.1.call-update) | async-done | bytes 1048592 | tf_op jit(solution)/shard_map/psum | solution.py:251
  967.2 92.2 %reduce-scatter.26.cloned.1.call-done = bf16[1,384,2048]{2,1,0:T(8,128)(2,1)} async-done(((bf16[8,384,2048]{2,1,0:T(8,128)(2,1)}), bf16[1,384,2048]{2,1,0:T(8,128)(2,1)}) %reduce-scatter.26.cloned.1.call-update) | async-done | bytes 1572880 | tf_op jit(solution)/shard_map/reduce_scatter | solution.py:204
  1061.2 93.8 %reduce-scatter.24.cloned.1.call-done = bf16[1,384,2048]{2,1,0:T(8,128)(2,1)} async-done(((bf16[8,384,2048]{2,1,0:T(8,128)(2,1)}), bf16[1,384,2048]{2,1,0:T(8,128)(2,1)}) %reduce-scatter.24.cloned.1.call-update) | async-done | bytes 1572880 | tf_op jit(solution)/shard_map/reduce_scatter | solution.py:204
  1159.1 91.7 %reduce-scatter.22.cloned.1.call-done = bf16[1,384,2048]{2,1,0:T(8,128)(2,1)} async-done(((bf16[8,384,2048]{2,1,0:T(8,128)(2,1)}), bf16[1,384,2048]{2,1,0:T(8,128)(2,1)}) %reduce-scatter.22.cloned.1.call-update) | async-done | bytes 1572880 | tf_op jit(solution)/shard_map/reduce_scatter | solution.py:204
  1254.8 91.8 %reduce-scatter.20.cloned.1.call-done = bf16[1,384,2048]{2,1,0:T(8,128)(2,1)} async-done(((bf16[8,384,2048]{2,1,0:T(8,128)(2,1)}), bf16[1,384,2048]{2,1,0:T(8,128)(2,1)}) %reduce-scatter.20.cloned.1.call-update) | async-done | bytes 1572880 | tf_op jit(solution)/shard_map/reduce_scatter | solution.py:204
  1356.3 59.4 %all-gather.37.cloned.1.call-done = bf16[1024,1664]{0,1:T(8,128)(2,1)} async-done(((bf16[256,1664]{0,1:T(8,128)(2,1)}), bf16[1024,1664]{0,1:T(8,128)(2,1)}) %all-gather.37.cloned.1.call-update) | async-done | bytes 3407888 | tf_op jit(solution)/shard_map/all_gather | solution.py:298
  1433.4 8.7 copy.156
  (411 shorter events, 327.2 us)
Async XLA Ops:
  7.2 50.8 %all-gather.25.cloned.1.call-start = ((), (), s32[]{:S(2)}) async-start(), calls=%async_computation.24 | async-start | bytes 2621440 | tf_op jit(solution)/shard_map/all_gather | solution.py:94
  7.9 100.2 %all-gather.19.cloned.1.call-start = ((), (), s32[]{:S(2)}) async-start(), calls=%async_computation.11 | async-start | bytes 7667712 | tf_op jit(solution)/shard_map/all_gather | solution.py:110
  13.8 94.4 %copy-start.73 = (bf16[8,128]{1,0:T(8,128)(2,1)S(1)}, bf16[8,128]{1,0:T(8,128)(2,1)}, u32[]{:S(2)}) copy-start(bf16[8,128]{1,0:T(8,128)(2,1)} %constant.61.clone) | copy-start | bytes 6148
  14.9 149.4 %all-gather.21.cloned.1.call-start = ((), (), s32[]{:S(2)}) async-start(), calls=%async_computation.12 | async-start | bytes 9437184 | tf_op jit(solution)/shard_map/all_gather | solution.py:111
  15.7 201.6 %all-gather.23.cloned.1.call-start = ((), (), s32[]{:S(2)}) async-start(), calls=%async_computation.13 | async-start | bytes 2621440 | tf_op jit(solution)/shard_map/all_gather | solution.py:163
  18.4 106.8 %copy-start.28 = (f32[512,64]{1,0:T(8,128)}, f32[512,64]{1,0:T(8,128)S(1)}, u32[]{:S(2)}) copy-start(f32[512,64]{1,0:T(8,128)S(1)} %get-tuple-element.81) | copy-start | bytes 393220
  60.1 49.4 %copy-start.74 = (f32[512]{0:T(512)}, f32[512]{0:T(512)S(1)}, u32[]{:S(2)}) copy-start(f32[512]{0:T(512)S(1)} %add_rsqrt_fusion.2) | copy-start | bytes 6148
  109.5 59.8 %copy-start.53 = (f32[1,2048]{1,0:T(1,128)}, f32[1,2048]{1,0:T(1,128)S(1)}, u32[]{:S(2)}) copy-start(f32[1,2048]{1,0:T(1,128)S(1)} %get-tuple-element.77) | copy-start | bytes 24580
  171.2 119.2 %all-gather.31.cloned.1.call-start = ((), (), s32[]{:S(2)}) async-start(), calls=%async_computation.27 | async-start | bytes 14155776 | tf_op jit(solution)/shard_map/all_gather | solution.py:114
  175.8 189.0 %all-gather.27.cloned.1.call-start = ((), (), s32[]{:S(2)}) async-start(), calls=%async_computation.25 | async-start | bytes 14155776 | tf_op jit(solution)/shard_map/all_gather | solution.py:114
  178.2 260.5 %all-gather.29.cloned.1.call-start = ((), (), s32[]{:S(2)}) async-start(), calls=%async_computation.26 | async-start | bytes 14155776 | tf_op jit(solution)/shard_map/all_gather | solution.py:114
  180.8 331.8 %all-gather.33.cloned.1.call-start = ((), (), s32[]{:S(2)}) async-start(), calls=%async_computation.28 | async-start | bytes 14155776 | tf_op jit(solution)/shard_map/all_gather | solution.py:114
  182.1 377.8 %all-gather.35.cloned.1.call-start = ((), (), s32[]{:S(2)}) async-start(), calls=%async_computation.29 | async-start | bytes 2621440 | tf_op jit(solution)/shard_map/all_gather | solution.py:112
  182.9 489.4 %reduce-scatter.12.cloned.1.call-start = ((), (), s32[]{:S(2)}) async-start(), calls=%async_computation.15 | async-start | bytes 2785280 | tf_op jit(solution)/shard_map/reduce_scatter | solution.py:215
  196.9 102.0 %copy-start.49 = (pred[512,16]{1,0:T(8,128)(4,1)}, pred[512,16]{1,0:T(8,128)(4,1)S(1)}, u32[]{:S(2)}) copy-start(pred[512,16]{1,0:T(8,128)(4,1)S(1)} %copy.136) | copy-start | bytes 24580
  220.2 78.6 %copy-start.64 = (f32[512]{0:T(512)}, f32[512]{0:T(512)S(1)}, u32[]{:S(2)}) copy-start(f32[512]{0:T(512)S(1)} %get-tuple-element.25) | copy-start | bytes 6148
  583.2 53.8 %copy-start.78 = (bf16[512,1024]{1,0:T(8,128)(2,1)}, bf16[512,1024]{1,0:T(8,128)(2,1)S(1)}, u32[]{:S(2)}) copy-start(bf16[512,1024]{1,0:T(8,128)(2,1)S(1)} %get-tuple-element.39) | copy-start | bytes 3145732
  626.8 91.3 %reduce-scatter.10.cloned.1.call-start = ((), (), s32[]{:S(2)}) async-start(), calls=%async_computation.14 | async-start | bytes 2621440 | tf_op jit(solution)/shard_map/reduce_scatter | solution.py:223
  637.1 37.4 %copy-start.46 = (f32[512,16]{1,0:T(8,128)S(1)}, f32[512,16]{1,0:T(8,128)}, u32[]{:S(2)}) copy-start(f32[512,16]{1,0:T(8,128)} %copy-done.45) | copy-start | bytes 98308
  640.9 34.6 %copy-start.71 = (f32[128]{0:T(128)S(1)}, f32[128]{0:T(128)}, u32[]{:S(2)}) copy-start(f32[128]{0:T(128)} %copy-done.70) | copy-start | bytes 1540
  640.9 77.1 %copy-start.35 = (bf16[1,128,2048]{2,1,0:T(8,128)(2,1)S(1)}, bf16[1,128,2048]{2,1,0:T(8,128)(2,1)}, u32[]{:S(2)}) copy-start(bf16[1,128,2048]{2,1,0:T(8,128)(2,1)} %param.15) | copy-start | bytes 1572868
  640.9 156.3 %reduce-scatter.18.cloned.1.call-start = ((), (), s32[]{:S(2)}) async-start(), calls=%async_computation.18 | async-start | bytes 9437184 | tf_op jit(solution)/shard_map/reduce_scatter | solution.py:248
  674.4 46.2 %copy-start.9 = (bf16[128,4,4,128]{0,3,2,1:T(8,128)(2,1)S(1)}, bf16[128,4,4,128]{0,3,2,1:T(8,128)(2,1)}, u32[]{:S(2)}) copy-start(bf16[128,4,4,128]{0,3,2,1:T(8,128)(2,1)} %copy-done.8) | copy-start | bytes 1572868
  733.7 17.9 %all-to-all-start.1 = ((bf16[128,16,128]{2,0,1:T(8,128)(2,1)}), bf16[128,16,128]{2,0,1:T(8,128)(2,1)S(1)}, u32[]{:S(2)}, u32[]{:S(2)}) async-start(bf16[128,16,128]{2,0,1:T(8,128)(2,1)} %bitcast.281), calls=%async_computation.3 | async-start | bytes 1048576 | tf_op jit(solution)/shard_map/all_to_all | solution.py:246
  737.2 137.6 %reduce-scatter.16.cloned.1.call-start = ((), (), s32[]{:S(2)}) async-start(), calls=%async_computation.17 | async-start | bytes 7667712 | tf_op jit(solution)/shard_map/reduce_scatter | solution.py:292
  792.0 119.2 %reduce-scatter.14.cloned.1.call-start = ((), (), s32[]{:S(2)}) async-start(), calls=%async_computation.16 | async-start | bytes 2621440 | tf_op jit(solution)/shard_map/reduce_scatter | solution.py:270
  792.5 171.9 %all-reduce.9.cloned.1.call-start = ((), (), s32[]{:S(2)}) async-start(), calls=%async_computation.19 | async-start | bytes 2097152 | tf_op jit(solution)/shard_map/psum | solution.py:251
  797.3 262.1 %reduce-scatter.26.cloned.1.call-start = ((), (), s32[]{:S(2)}) async-start(), calls=%async_computation.23 | async-start | bytes 14155776 | tf_op jit(solution)/shard_map/reduce_scatter | solution.py:204
  816.0 339.0 %reduce-scatter.24.cloned.1.call-start = ((), (), s32[]{:S(2)}) async-start(), calls=%async_computation.22 | async-start | bytes 14155776 | tf_op jit(solution)/shard_map/reduce_scatter | solution.py:204
  835.6 415.1 %reduce-scatter.22.cloned.1.call-start = ((), (), s32[]{:S(2)}) async-start(), calls=%async_computation.21 | async-start | bytes 14155776 | tf_op jit(solution)/shard_map/reduce_scatter | solution.py:204
  855.3 491.3 %reduce-scatter.20.cloned.1.call-start = ((), (), s32[]{:S(2)}) async-start(), calls=%async_computation.20 | async-start | bytes 14155776 | tf_op jit(solution)/shard_map/reduce_scatter | solution.py:204
  874.7 541.0 %all-gather.37.cloned.1.call-start = ((), (), s32[]{:S(2)}) async-start(), calls=%async_computation.30 | async-start | bytes 4259840 | tf_op jit(solution)/shard_map/all_gather | solution.py:298
  (95 other events, 576.1 us)
Sparse Core Ops, SparseCore 0:
  9.6 48.3 all-gather.24
  60.4 47.6 all-gather.18
  110.1 54.2 all-gather.20
  171.3 45.9 all-gather.22
  219.6 70.7 all-gather.30
  292.8 71.9 all-gather.26
  366.7 71.9 all-gather.28
  440.6 71.9 all-gather.32
  514.2 45.6 all-gather.34
  626.9 45.2 reduce-scatter.11
  675.1 42.8 reduce-scatter.9
  726.5 70.7 reduce-scatter.17
  800.7 64.0 reduce-scatter.15
  867.5 43.6 reduce-scatter.13
  913.3 51.0 all-reduce.8
  967.8 91.5 reduce-scatter.25
  1062.7 92.2 reduce-scatter.23
  1158.4 92.2 reduce-scatter.21
  1254.2 92.2 reduce-scatter.19
  1348.0 67.6 all-gather.36
